TPU v7x, 32 devices: a whole 2x2x4 slice. The times are simulated.
32 devices in a mesh: batch: 8 (over z, y), mp: 4 (over x, core).
Axes of the slice: x: 2, y: 2, z: 4, core: 2. Of those that a mesh axis runs over, the one named last changes fastest.
Arguments:
- init_state: float32 [4096, 256], P(('batch', 'mp')), may hold values from -6 to 6
- brownian: bfloat16 [32, 4096, 256], P(None, ('batch', 'mp')), may hold values from -6 to 6
- step_size: float32 [4096], P(('batch', 'mp')), may hold values from 0.02 to 0.1
- lengths: int32 [4096], P(('batch', 'mp')), may hold values from 1 to 32, as said below
- obs_steps: int32 [4096, 8], P(('batch', 'mp')), may hold values from 1 to 32, as said below
- observed: bfloat16 [4096, 8, 128], P(('batch', 'mp')), may hold values from -6 to 6
- w_in: bfloat16 [256, 1024], P(None, 'mp'), may hold values from -0.375 to 0.375
- b_in: bfloat16 [1024], P('mp'), may hold values from -3 to 3
- w_out: bfloat16 [1024, 256], P('mp'), may hold values from -0.1875 to 0.1875
- b_out: float32 [256], replicated, may hold values from -4 to 4
- decoder: bfloat16 [256, 128], replicated, may hold values from -0.375 to 0.375
- prior_rate: float32 [256], replicated, may hold values from 0.1 to 2
- diffusion: float32 [256], replicated, may hold values from 0.7 to 1.4
Outputs:
- elbo_series: float32 [4096], P(('batch', 'mp'))
- scores: float32 [2], replicated
- grad_w_in: float32 [256, 1024], P(None, 'mp')
- grad_b_in: float32 [1024], P('mp')
- grad_w_out: float32 [1024, 256], P('mp')
- grad_b_out: float32 [256], replicated
- grad_decoder: float32 [256, 128], replicated
- grad_init: float32 [4096, 256], P(('batch', 'mp'))
Inputs may be any that keep to these rules, and one draw needn't show every extreme that they name: `lengths`: some series has 32 live steps in every draw. obs_steps[i, j] is at most lengths[i].
All inputs are finite; a program needn't handle non-finite values.
Results may differ from a plain program's by a relative error of at most 0.0019.
Values may be sent and summed in bfloat16 or wider, within the bound.
A program may use at most 64 MiB of HBM per device.

v0:
```python
import jax
import jax.numpy as jnp
from jax import lax
from jax.sharding import PartitionSpec as P


def solve(
    init_state,
    brownian,
    step_size,
    lengths,
    obs_steps,
    observed,
    horizon,
    w_in_all,
    b_in_all,
    w_out_all,
    b_out,
    decoder,
    prior_rate,
    diffusion,
):
    row_count = init_state.shape[0]
    num_steps = brownian.shape[0]
    latent_width = init_state.shape[1]
    hidden_width = w_in_all.shape[1]
    step_col = step_size[:, None]
    root_col = jnp.sqrt(step_size)[:, None]
    bias_in = b_in_all.astype(jnp.float32)

    def forward(step_index, loop_state):
        trajectory, activities, residuals, kl_sum = loop_state
        current = lax.dynamic_index_in_dim(trajectory, step_index, 0, keepdims=False)
        increment = lax.dynamic_index_in_dim(brownian, step_index, 0, keepdims=False)
        live_now = (step_index < lengths).astype(jnp.float32)
        activity = jnp.tanh(
            jnp.dot(current.astype(jnp.bfloat16), w_in_all, preferred_element_type=jnp.float32)
            + bias_in
        ).astype(jnp.bfloat16)
        drift_now = jnp.dot(activity, w_out_all, preferred_element_type=jnp.float32) + b_out
        residual = (drift_now + prior_rate * current) / diffusion
        kl_sum = kl_sum + live_now * 0.5 * step_size * jnp.sum(residual * residual, axis=1)
        following = current + live_now[:, None] * (
            step_col * drift_now + diffusion * root_col * increment.astype(jnp.float32)
        )
        trajectory = lax.dynamic_update_index_in_dim(trajectory, following, step_index + 1, 0)
        activities = lax.dynamic_update_index_in_dim(activities, activity, step_index, 0)
        residuals = lax.dynamic_update_index_in_dim(residuals, residual, step_index, 0)
        return (trajectory, activities, residuals, kl_sum)

    start_path = lax.dynamic_update_index_in_dim(
        jnp.zeros((num_steps + 1, row_count, latent_width), jnp.float32), init_state, 0, 0
    )
    start_forward = (
        start_path,
        jnp.zeros((num_steps, row_count, hidden_width), jnp.bfloat16),
        jnp.zeros((num_steps, row_count, latent_width), jnp.float32),
        jnp.zeros((row_count,), jnp.float32),
    )
    trajectory, activities, residuals, kl_total = lax.fori_loop(0, horizon, forward, start_forward)
    picked = trajectory[obs_steps, jnp.arange(row_count, dtype=jnp.int32)[:, None]]
    picked_round = picked.astype(jnp.bfloat16).reshape(-1, latent_width)
    flat_obs = observed.reshape(-1, observed.shape[2]).astype(jnp.float32)
    misfit = jnp.dot(picked_round, decoder, preferred_element_type=jnp.float32) - flat_obs
    loglik = -0.5 * jnp.sum((misfit * misfit).reshape(row_count, -1), axis=1)
    misfit_round = misfit.astype(jnp.bfloat16)
    decoder_grad = jnp.dot(picked_round.T, misfit_round, preferred_element_type=jnp.float32)
    misfit_back = jnp.dot(misfit_round, decoder.T, preferred_element_type=jnp.float32).reshape(
        row_count, obs_steps.shape[1], latent_width
    )
    onehot = (
        obs_steps[:, :, None] == jnp.arange(num_steps + 1, dtype=jnp.int32)[None, None, :]
    ).astype(jnp.float32)
    obs_back = jnp.einsum("bjs,bjl->sbl", onehot, misfit_back, precision=lax.Precision.HIGHEST)

    def backward(back_index, loop_state):
        cotangent, sum_w_in, sum_b_in, sum_w_out, sum_b_out = loop_state
        step_index = horizon - 1 - back_index
        current = lax.dynamic_index_in_dim(trajectory, step_index, 0, keepdims=False)
        activity = lax.dynamic_index_in_dim(activities, step_index, 0, keepdims=False)
        residual = lax.dynamic_index_in_dim(residuals, step_index, 0, keepdims=False)
        obs_here = lax.dynamic_index_in_dim(obs_back, step_index, 0, keepdims=False)
        live_now = (step_index < lengths).astype(jnp.float32)
        factor = (live_now * step_size)[:, None]
        scaled = residual / diffusion
        update = factor * (cotangent + scaled)
        update_round = update.astype(jnp.bfloat16)
        activity_value = activity.astype(jnp.float32)
        pre_grad = jnp.dot(update_round, w_out_all.T, preferred_element_type=jnp.float32) * (
            1.0 - activity_value * activity_value
        )
        pre_round = pre_grad.astype(jnp.bfloat16)
        cotangent = (
            cotangent
            + factor * prior_rate * scaled
            + jnp.dot(pre_round, w_in_all.T, preferred_element_type=jnp.float32)
            + obs_here
        )
        sum_w_in = sum_w_in + jnp.dot(
            current.astype(jnp.bfloat16).T, pre_round, preferred_element_type=jnp.float32
        )
        sum_b_in = sum_b_in + jnp.sum(pre_grad, axis=0)
        sum_w_out = sum_w_out + jnp.dot(
            activity.T, update_round, preferred_element_type=jnp.float32
        )
        sum_b_out = sum_b_out + jnp.sum(update, axis=0)
        return (cotangent, sum_w_in, sum_b_in, sum_w_out, sum_b_out)

    start_back = (
        lax.dynamic_index_in_dim(obs_back, horizon, 0, keepdims=False),
        jnp.zeros((latent_width, hidden_width), jnp.float32),
        jnp.zeros((hidden_width,), jnp.float32),
        jnp.zeros((hidden_width, latent_width), jnp.float32),
        jnp.zeros((latent_width,), jnp.float32),
    )
    cotangent, sum_w_in, sum_b_in, sum_w_out, sum_b_out = lax.fori_loop(
        0, horizon, backward, start_back
    )
    divisor = (latent_width * lengths + observed.shape[2] * obs_steps.shape[1]).astype(jnp.float32)
    elbo_rows = (loglik - kl_total) / divisor
    return (
        elbo_rows,
        cotangent,
        jnp.sum(loglik),
        jnp.sum(kl_total),
        sum_w_in,
        sum_b_in,
        sum_w_out,
        sum_b_out,
        decoder_grad,
    )


def on_device(
    init_state,
    brownian,
    step_size,
    lengths,
    obs_steps,
    observed,
    w_in,
    b_in,
    w_out,
    b_out,
    decoder,
    prior_rate,
    diffusion,
):
    w_in_all, w_out_all, b_in_all = (
        lax.all_gather(w_in, "mp", axis=1, tiled=True),
        lax.all_gather(w_out, "mp", axis=0, tiled=True),
        lax.all_gather(b_in, "mp", axis=0, tiled=True),
    )
    row_count = init_state.shape[0]
    num_steps = brownian.shape[0]
    hidden_width = w_in_all.shape[1]
    shared = (w_in_all, b_in_all, w_out_all, b_out, decoder, prior_rate, diffusion)
    outcome = solve(
        init_state, brownian, step_size, lengths, obs_steps, observed, num_steps, *shared
    )
    (
        elbo_series,
        cotangent,
        loglik_local,
        kl_local,
        sum_w_in,
        sum_b_in,
        sum_w_out,
        sum_b_out,
        decoder_grad,
    ) = outcome
    loglik_all, kl_all = lax.psum((loglik_local, kl_local), ("batch", "mp"))
    total_series = row_count * lax.axis_size("batch") * lax.axis_size("mp")
    share = hidden_width // lax.axis_size("mp")
    offset = lax.axis_index("mp") * share
    all_w_in, all_b_in, all_w_out, all_b_out, all_decoder = lax.psum(
        (sum_w_in, sum_b_in, sum_w_out, sum_b_out, decoder_grad), ("batch", "mp")
    )
    own_w_in = lax.dynamic_slice_in_dim(all_w_in, offset, share, 1)
    own_b_in = lax.dynamic_slice_in_dim(all_b_in, offset, share, 0)
    own_w_out = lax.dynamic_slice_in_dim(all_w_out, offset, share, 0)
    scores = jnp.stack([loglik_all / total_series, kl_all / total_series])
    return (
        elbo_series,
        scores,
        own_w_in / total_series,
        own_b_in / total_series,
        own_w_out / total_series,
        all_b_out / total_series,
        all_decoder / total_series,
        cotangent,
    )


def solution(mesh):
    placed = (
        P(("batch", "mp"), None),
        P(None, ("batch", "mp"), None),
        P(("batch", "mp")),
        P(("batch", "mp")),
        P(("batch", "mp"), None),
        P(("batch", "mp"), None, None),
        P(None, "mp"),
        P("mp"),
        P("mp", None),
        P(),
        P(),
        P(),
        P(),
    )
    return jax.shard_map(
        on_device,
        mesh=mesh,
        in_specs=placed,
        out_specs=(
            P(("batch", "mp")),
            P(),
            P(None, "mp"),
            P("mp"),
            P("mp", None),
            P(),
            P(),
            P(("batch", "mp"), None),
        ),
        check_vma=False,
    )
```

profile of v0, /device:TPU:0, one launch (start us, length us, event | category | flops | bytes accessed | tf_op | source)
XLA Modules:
  0.0 919.2 jit_solution(16024416329355499509)
XLA Ops:
  8.8 8.9 all_gather.11
  17.7 7.5 all_gather.9
  25.8 5.1 all-gather
  31.5 3.4 dynamic_update_slice.37
  34.9 372.4 %while.46 = (s32[]{:T(128)}, f32[33,128,256]{2,1,0:T(8,128)}, bf16[32,128,1024]{2,1,0:T(8,128)(2,1)}, f32[32,128,256]{2,1,0:T(8,128)}, f32[128]{0:T(128)}, /*ind...) while((s32[]{:T(128)}, f32[33,128,256]{2,1,0:T(8,128)}, ...), condition=%wide.region_2.3_spmd.clone, body=%wide.region_0.2_spmd.clone.sunk | while | flops 135005056 | bytes 20398324 | solution.py:60
  38.4 2.2 copy.43
  43.4 2.0 copy.55
  50.0 2.2 copy.43
  55.0 2.0 copy.55
  61.6 2.2 copy.43
  73.2 2.2 copy.43
  84.9 2.2 copy.43
  96.5 2.2 copy.43
  108.2 2.2 copy.43
  119.8 2.2 copy.43
  131.4 2.2 copy.43
  143.1 2.2 copy.43
  154.7 2.2 copy.43
  166.4 2.2 copy.43
  178.0 2.2 copy.43
  189.7 2.2 copy.43
  201.3 2.2 copy.43
  212.9 2.2 copy.43
  224.5 2.2 copy.43
  236.1 2.2 copy.43
  247.8 2.2 copy.43
  259.4 2.2 copy.43
  271.0 2.2 copy.43
  282.7 2.2 copy.43
  294.3 2.2 copy.43
  306.0 2.2 copy.43
  317.6 2.2 copy.43
  329.3 2.2 copy.43
  340.9 2.2 copy.43
  352.6 2.2 copy.43
  364.2 2.2 copy.43
  375.8 2.2 copy.43
  387.4 2.2 copy.43
  399.1 2.2 copy.43
  407.5 3.9 convert.36
  411.4 17.4 %gather_fusion = bf16[1024,256]{1,0:T(8,128)(2,1)} fusion(f32[33,128,256]{2,1,0:T(8,128)} %get-tuple-element.954, s32[1024]{0:T(1024)S(1)} %reshape.63), kind=kCustom, calls=%fused_computation | custom fusion | bytes 1056768 | tf_op jit(solution)/shard_map/gather | solution.py:61
  429.7 2.1 copy.29
  431.8 2.1 multiply_reduce_fusion.1
  434.2 2.0 fusion.25
  436.3 2.9 fusion.23
  441.6 327.9 %while.47 = (s32[]{:T(128)}, f32[128,256]{1,0:T(8,128)}, f32[256,1024]{1,0:T(8,128)S(1)}, f32[1024]{0:T(1024)S(1)}, f32[1024,256]{1,0:T(8,128)S(1)}, /*index=5*/...) while((s32[]{:T(128)}, f32[128,256]{1,0:T(8,128)}, ...), condition=%wide.region_12.13_spmd.clone, body=%wide.region_9.12_spmd.clone.sunk | while | flops 270632448 | bytes 7899009 | solution.py:116
  773.5 41.0 %all-reduce.1 = (f32[]{:T(128)}, f32[]{:T(128)}, f32[1024]{0:T(1024)S(1)}, f32[256]{0:T(256)S(1)}) all-reduce(f32[]{:T(128)} %get-tuple-element.1005, f32[]{:T(128)} %get-tuple-element.1003, f32[1024]{0:T(1024)S(1)} %get-tuple-element.769, f32[256]{0:T(256)} %get-tuple-element.771), channel_id=1, replica_groups=mesh['batch'=8,'mp'=4] {'batch','mp'}, use_global_device_ids=true, to_apply=%region_8.9 | all-reduce | flops 1282 | bytes 10256 | tf_op jit(solution)/shard_map/psum | solution.py:172
  817.1 91.8 %all-reduce.5.cloned.1.call-done = (f32[256,1024]{1,0:T(8,128)}, f32[1024,256]{1,0:T(8,128)}, f32[256,128]{1,0:T(8,128)}) async-done(((f32[256,1024]{1,0:T(8,128)}, f32[1024,256]{1,0:T(8,128)}, f32[256,128]{1,0:T(8,128)}), (f32[256,1024]{1,0:T(8,128)}, f32[1024,256]{1,0:T(8,128)}, f32[256,128]{1,0:T(8,128)})) %all-reduce.5.cloned.1.call-update) | async-done | bytes 2228240 | tf_op jit(solution)/shard_map/psum | solution.py:176
  (745 shorter events, 637.5 us)
Async XLA Ops:
  7.2 424.6 %copy-start = (bf16[256,128]{1,0:T(8,128)(2,1)S(1)}, bf16[256,128]{1,0:T(8,128)(2,1)}, u32[]{:S(2)}) copy-start(bf16[256,128]{1,0:T(8,128)(2,1)} %param.27) | copy-start | bytes 196612
  7.2 27.7 %copy-start.10 = (f32[256]{0:T(256)S(1)}, f32[256]{0:T(256)}, u32[]{:S(2)}) copy-start(f32[256]{0:T(256)} %param.26) | copy-start | bytes 3076
  7.2 27.7 %copy-start.8 = (f32[256]{0:T(256)S(1)}, f32[256]{0:T(256)}, u32[]{:S(2)}) copy-start(f32[256]{0:T(256)} %param.28) | copy-start | bytes 3076
  7.2 27.7 %copy-start.5 = (f32[256]{0:T(256)S(1)}, f32[256]{0:T(256)}, u32[]{:S(2)}) copy-start(f32[256]{0:T(256)} %param.29) | copy-start | bytes 3076
  7.2 901.7 %all-reduce.5.cloned.1.call-start = ((), (), s32[]{:S(2)}) async-start(), calls=%async_computation | async-start | bytes 4456448 | tf_op jit(solution)/shard_map/psum | solution.py:176
  407.5 21.3 %copy-start.4 = (bf16[128,8,128]{2,1,0:T(8,128)(2,1)S(1)}, bf16[128,8,128]{2,1,0:T(8,128)(2,1)}, u32[]{:S(2)}) copy-start(bf16[128,8,128]{2,1,0:T(8,128)(2,1)} %param.22) | copy-start | bytes 786436
  454.2 4.0 copy-start.7
  464.5 4.0 copy-start.7
  464.5 4.0 copy-start.9
  474.7 4.0 copy-start.7
  485.0 4.0 copy-start.7
  485.0 4.0 copy-start.9
  495.3 4.0 copy-start.7
  505.5 4.0 copy-start.7
  505.5 4.0 copy-start.9
  515.8 4.0 copy-start.7
  526.1 4.0 copy-start.7
  526.1 4.0 copy-start.9
  536.4 4.0 copy-start.7
  546.6 4.0 copy-start.7
  546.6 4.0 copy-start.9
  556.9 4.0 copy-start.7
  567.2 4.0 copy-start.7
  567.2 4.0 copy-start.9
  577.4 4.0 copy-start.7
  587.7 4.0 copy-start.7
  587.7 4.0 copy-start.9
  598.0 4.0 copy-start.7
  608.2 4.0 copy-start.7
  608.2 4.0 copy-start.9
  618.5 4.0 copy-start.7
  628.8 4.0 copy-start.7
  628.8 4.0 copy-start.9
  639.0 4.0 copy-start.7
  649.3 4.0 copy-start.7
  649.3 4.0 copy-start.9
  669.8 4.0 copy-start.7
  669.9 4.0 copy-start.9
  680.1 4.0 copy-start.7
  690.4 4.0 copy-start.7
  690.4 4.0 copy-start.9
  710.9 4.0 copy-start.7
  710.9 4.0 copy-start.9
  731.5 4.0 copy-start.7
  731.5 4.0 copy-start.9
  741.7 4.0 copy-start.7
  752.0 4.0 copy-start.7
  752.0 4.0 copy-start.9
  (57 other events, 127.2 us)
Sparse Core Ops, SparseCore 0:
  771.0 137.9 all-reduce.4
where the time goes:
time: 932 us; the launch traced here: 919 us
  matrix products  310 us (33%)
  local copies, waits for them, and re-layouts  237 us (25%)
  other arithmetic  199 us (21%)
  waiting for transfers between devices  91.8 us (10%)
  blocking collectives  62.4 us (7%)
  between operations  15.5 us (2%)
    while x256, local copies, waits for them, and re-layouts  136 us
    psum x1, waiting for transfers between devices, on_device(): lax.psum((sum_w_in, sum_b_in, sum_w_out, sum_b_out, decoder_grad), ('batc...  91.8 us
    dot_general x32, matrix products, backward(): jnp.dot(pre_round, w_in_all.T, preferred_element_type=jnp.float32)  62.3 us
    dot_general x32, matrix products, forward(): jnp.dot(current.astype(jnp.bfloat16), w_in_all, preferred_element_type=jn...  59.5 us
    dot_general x32, matrix products, forward(): jnp.dot(activity, w_out_all, preferred_element_type=jnp.float32) + b_out  55.7 us
    dot_general x32, matrix products, backward(): jnp.dot(activity.T, update_round, preferred_element_type=jnp.float32)  44.8 us
    dynamic_slice x32, local copies, waits for them, and re-layouts, backward(): obs_here = lax.dynamic_index_in_dim(obs_back, step_index, 0, keepdims=False)  42.4 us
    psum x1, blocking collectives, on_device(): loglik_all, kl_all = lax.psum((loglik_local, kl_local), ('batch', 'mp'))  41 us
  transfers between devices with their start and end apart: 1, of which 1 were waited for; matrix products, arithmetic and copies ran while one was open for 0% of the time, Pallas kernels for 0%

commit v1 on v0

--- a/solution.py
+++ b/solution.py
@@ -174,7 +174,7 @@
     share = hidden_width // lax.axis_size("mp")
     offset = lax.axis_index("mp") * share
     all_w_in, all_b_in, all_w_out, all_b_out, all_decoder = lax.psum(
-        (sum_w_in, sum_b_in, sum_w_out, sum_b_out, decoder_grad), ("batch", "mp")
+        lax.psum((sum_w_in, sum_b_in, sum_w_out, sum_b_out, decoder_grad), "batch"), "mp"
     )
     own_w_in = lax.dynamic_slice_in_dim(all_w_in, offset, share, 1)
     own_b_in = lax.dynamic_slice_in_dim(all_b_in, offset, share, 0)

time: 932 us -> 973 us (1.044)
  blocking collectives: 62.4 us -> 89.3 us
  waiting for transfers between devices: 91.8 us -> 107 us
    psum x0 -> x2, blocking collectives: none -> 27.5 us  [the longest x1 21.5 us: on_device(): lax.psum((sum_w_in, sum_b_in, sum_w_out, sum_b_out, decoder_grad), 'batch')]
    psum x1 -> x2, waiting for transfers between devices: 91.8 us -> 107 us  [the longest x1 107 us: on_device(): lax.psum((sum_w_in, sum_b_in, sum_w_out, sum_b_out, decoder_grad), 'batch')]
  transfers between devices with their start and end apart: 1 -> 2, of which waited for: 1 -> 1; matrix products, arithmetic and copies ran while one was open for 0% -> 0% of each run, Pallas kernels for 0% -> 0%
where the time goes in v1:
time: 973 us; the launch traced here: 961 us
  matrix products  310 us (32%)
  local copies, waits for them, and re-layouts  237 us (24%)
  other arithmetic  199 us (20%)
  waiting for transfers between devices  107 us (11%)
  blocking collectives  89.3 us (9%)
  between operations  15.5 us (2%)
    while x256, local copies, waits for them, and re-layouts  136 us
    psum x1, waiting for transfers between devices, on_device(): lax.psum((sum_w_in, sum_b_in, sum_w_out, sum_b_out, decoder_grad), 'batch')  107 us
    dot_general x32, matrix products, backward(): jnp.dot(pre_round, w_in_all.T, preferred_element_type=jnp.float32)  62.3 us
    dot_general x32, matrix products, forward(): jnp.dot(current.astype(jnp.bfloat16), w_in_all, preferred_element_type=jn...  59.4 us
    dot_general x32, matrix products, forward(): jnp.dot(activity, w_out_all, preferred_element_type=jnp.float32) + b_out  55.6 us
    dot_general x32, matrix products, backward(): jnp.dot(activity.T, update_round, preferred_element_type=jnp.float32)  44.8 us
    dynamic_slice x32, local copies, waits for them, and re-layouts, backward(): obs_here = lax.dynamic_index_in_dim(obs_back, step_index, 0, keepdims=False)  42.4 us
    dot_general x32, matrix products, backward(): jnp.dot(update_round, w_out_all.T, preferred_element_type=jnp.float32)  40.7 us
  transfers between devices with their start and end apart: 2, of which 1 were waited for; matrix products, arithmetic and copies ran while one was open for 0% of the time, Pallas kernels for 0%

profile of v1, /device:TPU:0, one launch (start us, length us, event | category | flops | bytes accessed | tf_op | source)
XLA Modules:
  0.0 960.8 jit_solution(6265119509140694065)
XLA Ops:
  8.8 8.9 all_gather.11
  17.7 7.5 all_gather.9
  25.8 5.1 all-gather
  31.5 3.4 dynamic_update_slice.37
  34.9 372.3 %while.46 = (s32[]{:T(128)}, f32[33,128,256]{2,1,0:T(8,128)}, bf16[32,128,1024]{2,1,0:T(8,128)(2,1)}, f32[32,128,256]{2,1,0:T(8,128)}, f32[128]{0:T(128)}, /*ind...) while((s32[]{:T(128)}, f32[33,128,256]{2,1,0:T(8,128)}, ...), condition=%wide.region_2.3_spmd.clone, body=%wide.region_0.2_spmd.clone.sunk | while | flops 135005056 | bytes 20398324 | solution.py:60
  38.4 2.2 copy.43
  50.0 2.2 copy.43
  61.6 2.2 copy.43
  73.3 2.2 copy.43
  84.9 2.2 copy.43
  96.5 2.2 copy.43
  108.2 2.2 copy.43
  119.8 2.2 copy.43
  131.5 2.2 copy.43
  143.1 2.2 copy.43
  154.7 2.2 copy.43
  166.4 2.2 copy.43
  178.0 2.2 copy.43
  189.6 2.2 copy.43
  201.3 2.2 copy.43
  212.9 2.2 copy.43
  224.5 2.2 copy.43
  236.1 2.2 copy.43
  247.8 2.2 copy.43
  259.4 2.2 copy.43
  271.1 2.2 copy.43
  282.7 2.2 copy.43
  294.3 2.2 copy.43
  306.0 2.2 copy.43
  317.6 2.2 copy.43
  329.2 2.2 copy.43
  340.9 2.2 copy.43
  352.5 2.2 copy.43
  364.2 2.2 copy.43
  375.8 2.2 copy.43
  387.4 2.2 copy.43
  399.0 2.2 copy.43
  407.4 3.9 convert.36
  411.4 17.3 %gather_fusion = bf16[1024,256]{1,0:T(8,128)(2,1)} fusion(f32[33,128,256]{2,1,0:T(8,128)} %get-tuple-element.954, s32[1024]{0:T(1024)S(1)} %reshape.63), kind=kCustom, calls=%fused_computation | custom fusion | bytes 1056768 | tf_op jit(solution)/shard_map/gather | solution.py:61
  429.6 2.1 copy.29
  431.7 2.1 multiply_reduce_fusion.1
  434.1 2.0 fusion.25
  436.2 2.9 fusion.23
  441.5 327.9 %while.47 = (s32[]{:T(128)}, f32[128,256]{1,0:T(8,128)}, f32[256,1024]{1,0:T(8,128)S(1)}, f32[1024]{0:T(1024)S(1)}, f32[1024,256]{1,0:T(8,128)S(1)}, /*index=5*/...) while((s32[]{:T(128)}, f32[128,256]{1,0:T(8,128)}, ...), condition=%wide.region_12.13_spmd.clone, body=%wide.region_9.12_spmd.clone.sunk | while | flops 270632448 | bytes 7899009 | solution.py:116
  770.8 107.3 %all-reduce.9.cloned.1.call-done = (f32[256,1024]{1,0:T(8,128)}, f32[1024,256]{1,0:T(8,128)}, f32[256,128]{1,0:T(8,128)}) async-done(((f32[256,1024]{1,0:T(8,128)}, f32[1024,256]{1,0:T(8,128)}, f32[256,128]{1,0:T(8,128)}), (f32[256,1024]{1,0:T(8,128)}, f32[1024,256]{1,0:T(8,128)}, f32[256,128]{1,0:T(8,128)})) %all-reduce.9.cloned.1.call-update) | async-done | bytes 2228240 | tf_op jit(solution)/shard_map/psum | solution.py:177
  880.1 40.4 %all-reduce.1 = (f32[]{:T(128)}, f32[]{:T(128)}) all-reduce(f32[]{:T(128)} %get-tuple-element.1010, f32[]{:T(128)} %get-tuple-element.1008), channel_id=1, replica_groups=mesh['batch'=8,'mp'=4] {'batch','mp'}, use_global_device_ids=true, to_apply=%region_8.9 | all-reduce | flops 2 | bytes 16 | tf_op jit(solution)/shard_map/psum | solution.py:172
  921.7 21.5 %all-reduce.2 = (f32[1024]{0:T(1024)S(1)}, f32[256]{0:T(256)S(1)}) all-reduce(f32[1024]{0:T(1024)S(1)} %get-tuple-element.769, f32[256]{0:T(256)} %get-tuple-element.771), channel_id=1, replica_groups=mesh['batch'=8,'mp'=4] {'batch'}, use_global_device_ids=true, to_apply=%region_15.16 | all-reduce | flops 1280 | bytes 10240 | tf_op jit(solution)/shard_map/psum | solution.py:177
  943.2 6.1 all-reduce.4
  (752 shorter events, 640.8 us)
Async XLA Ops:
  7.2 424.5 %copy-start = (bf16[256,128]{1,0:T(8,128)(2,1)S(1)}, bf16[256,128]{1,0:T(8,128)(2,1)}, u32[]{:S(2)}) copy-start(bf16[256,128]{1,0:T(8,128)(2,1)} %param.27) | copy-start | bytes 196612
  7.2 27.7 %copy-start.11 = (f32[256]{0:T(256)S(1)}, f32[256]{0:T(256)}, u32[]{:S(2)}) copy-start(f32[256]{0:T(256)} %param.26) | copy-start | bytes 3076
  7.2 27.7 %copy-start.8 = (f32[256]{0:T(256)S(1)}, f32[256]{0:T(256)}, u32[]{:S(2)}) copy-start(f32[256]{0:T(256)} %param.28) | copy-start | bytes 3076
  7.2 27.7 %copy-start.5 = (f32[256]{0:T(256)S(1)}, f32[256]{0:T(256)}, u32[]{:S(2)}) copy-start(f32[256]{0:T(256)} %param.29) | copy-start | bytes 3076
  7.2 870.8 %all-reduce.9.cloned.1.call-start = ((), (), s32[]{:S(2)}) async-start(), calls=%async_computation | async-start | bytes 4456448 | tf_op jit(solution)/shard_map/psum | solution.py:177
  407.4 21.3 %copy-start.4 = (bf16[128,8,128]{2,1,0:T(8,128)(2,1)S(1)}, bf16[128,8,128]{2,1,0:T(8,128)(2,1)}, u32[]{:S(2)}) copy-start(bf16[128,8,128]{2,1,0:T(8,128)(2,1)} %param.22) | copy-start | bytes 786436
  444.5 4.0 copy-start.7
  454.1 4.0 copy-start.7
  464.4 4.0 copy-start.7
  464.4 4.0 copy-start.9
  474.6 4.0 copy-start.7
  484.9 4.0 copy-start.7
  484.9 4.0 copy-start.9
  495.2 4.0 copy-start.7
  505.4 4.0 copy-start.7
  505.4 4.0 copy-start.9
  515.7 4.0 copy-start.7
  526.0 4.0 copy-start.7
  526.0 4.0 copy-start.9
  536.2 4.0 copy-start.7
  546.5 4.0 copy-start.7
  546.5 4.0 copy-start.9
  567.1 4.0 copy-start.7
  567.1 4.0 copy-start.9
  587.6 4.0 copy-start.7
  587.6 4.0 copy-start.9
  597.9 4.0 copy-start.7
  608.1 4.0 copy-start.7
  608.1 4.0 copy-start.9
  628.7 4.0 copy-start.7
  628.7 4.0 copy-start.9
  649.2 4.0 copy-start.7
  649.2 4.0 copy-start.9
  659.5 4.0 copy-start.7
  669.7 4.0 copy-start.7
  669.8 4.0 copy-start.9
  690.3 4.0 copy-start.7
  690.3 4.0 copy-start.9
  710.8 4.0 copy-start.7
  710.8 4.0 copy-start.9
  721.1 4.0 copy-start.7
  731.4 4.0 copy-start.7
  731.4 4.0 copy-start.9
  751.9 4.0 copy-start.7
  751.9 4.0 copy-start.9
  762.2 4.0 copy-start.7
  769.4 108.6 %copy-start.10 = (f32[1024]{0:T(1024)S(1)}, f32[1024]{0:T(1024)}, u32[]{:S(2)}) copy-start(f32[1024]{0:T(1024)} %get-tuple-element.1011) | copy-start | bytes 12292
  770.7 179.8 %all-reduce.11.cloned.1.call-start = ((), (), s32[]{:S(2)}) async-start(), calls=%async_computation.1 | async-start | bytes 4456448 | tf_op jit(solution)/shard_map/psum | solution.py:176
  (59 other events, 135.2 us)
Sparse Core Ops, SparseCore 0:
  770.8 107.1 all-reduce.8
  880.5 53.5 all-reduce.10
